TPU v7x, 32 devices: a whole 2x2x4 slice. The times are simulated.
32 devices in a mesh: groups: 2 (over y), ctx: 4 (over z), head: 2 (over x), rep: 2 (over core).
Axes of the slice: x: 2, y: 2, z: 4, core: 2. Of those that a mesh axis runs over, the one named last changes fastest.
Arguments:
- queries: bfloat16 [2048, 4096], P(('groups', 'ctx'), ('head', 'rep')), parts along dimension 0, may hold values from -24 to 24
- keys: bfloat16 [2048, 1024], P(('groups', 'ctx'), ('head', 'rep')), parts along dimension 0, may hold values from -6 to 6
- values: bfloat16 [2048, 1024], P(('groups', 'ctx'), ('head', 'rep')), parts along dimension 0, may hold values from -6 to 6
- span_order: int32 [8], replicated, may hold values from 0 to 7, as said below
Outputs:
- attended: bfloat16 [2048, 4096], P(('groups', 'ctx'), ('head', 'rep')), parts along dimension 0
There are 2 independent parts, one for each index of `groups`. A program takes and returns all parts, laid end to end along the dimension named above; an argument that names none is the same for every part. Nothing has to cross between parts.
Inputs may be any that keep to these rules, and one draw needn't show every extreme that they name: `span_order`: A permutation of the spans in which entries 2 d and 2 d + 1 are c and 7 - c for some c.
All inputs are finite; a program needn't handle non-finite values.
Results may differ from a plain program's by a relative error of at most 0.0047.
Values may be sent and summed in bfloat16 or wider, within the bound.
A program may use at most 64 MiB of HBM per device.

v0:
```python
import math
import jax
import jax.numpy as jnp
from jax import lax
from jax.sharding import PartitionSpec as P

HEAD_SIZE = 128
masked_score = -1e30


def lookup_positions(span_order, first_row, row_count, span_rows):
    row_ids = first_row + jnp.arange(row_count, dtype=jnp.int32)
    span_ids = row_ids // span_rows
    span_table = jnp.arange(span_order.shape[0], dtype=jnp.int32)
    span_starts = jnp.sum(
        jnp.where(span_ids[:, None] == span_table[None, :], span_order[None, :], 0), axis=1
    )
    return span_starts * span_rows + row_ids % span_rows


def source_partials(query_block, query_pos, key_group, value_group, key_pos, head_dim):
    score_scale = 1.0 / math.sqrt(head_dim)
    scores = (
        jnp.einsum("rhgd,cshd->crhgs", query_block, key_group, preferred_element_type=jnp.float32)
        * score_scale
    )
    allowed = (key_pos[:, None, :] <= query_pos[None, :, None])[:, :, None, None, :]
    masked = jnp.where(allowed, scores, masked_score)
    row_top = jnp.max(masked, axis=-1)
    weights = jnp.where(allowed, jnp.exp(masked - row_top[..., None]), 0.0)
    row_total = jnp.sum(weights, axis=-1)
    numerator = jnp.einsum(
        "crhgs,cshd->crhgd",
        weights.astype(jnp.bfloat16),
        value_group,
        preferred_element_type=jnp.float32,
    )
    partial_value = (numerator / jnp.maximum(row_total, 1.0)[..., None]).astype(jnp.bfloat16)
    return (partial_value, row_top, row_total)


def absorb(running, partial_value, row_top, row_total):
    run_top, run_total, run_sum = running
    new_top = jnp.maximum(run_top, row_top)
    rescale = jnp.exp(run_top - new_top)
    source_weight = row_total * jnp.exp(row_top - new_top)
    return (
        new_top,
        run_total * rescale + source_weight,
        run_sum * rescale[..., None] + source_weight[..., None] * partial_value.astype(jnp.float32),
    )


def shards(queries, keys, values, span_order):
    rows_here = queries.shape[0]
    span_rows = rows_here // 2
    head_dim = HEAD_SIZE
    kv_heads = keys.shape[1] // head_dim
    common_values = queries.shape[1] // keys.shape[1]
    my_index = lax.axis_index("ctx")
    own_pos = lookup_positions(span_order, my_index * rows_here, rows_here, span_rows)
    q_local = queries.reshape(rows_here, kv_heads, common_values, head_dim)
    initial = (
        jnp.full((rows_here, kv_heads, common_values), masked_score, jnp.float32),
        jnp.zeros((rows_here, kv_heads, common_values), jnp.float32),
        jnp.zeros((rows_here, kv_heads, common_values, head_dim), jnp.float32),
    )
    running = initial
    k_piece = lax.all_gather(keys, "ctx", axis=0, tiled=True)
    v_piece = lax.all_gather(values, "ctx", axis=0, tiled=True)
    shard_count = k_piece.shape[0] // rows_here
    per_turn = 2
    turn_count = shard_count // per_turn
    k_pos = lookup_positions(span_order, jnp.int32(0), k_piece.shape[0], span_rows)
    k_steps = k_piece.reshape(turn_count, per_turn, rows_here, kv_heads, head_dim)
    v_steps = v_piece.reshape(turn_count, per_turn, rows_here, kv_heads, head_dim)
    p_steps = k_pos.reshape(turn_count, per_turn, rows_here)

    def one_turn(carried, inputs_now):
        partial_value, row_top, row_total = source_partials(
            q_local, own_pos, inputs_now[0], inputs_now[1], inputs_now[2], head_dim
        )
        for member in range(per_turn):
            carried = absorb(carried, partial_value[member], row_top[member], row_total[member])
        return (carried, None)

    running, unused = lax.scan(one_turn, running, (k_steps, v_steps, p_steps))
    merged = running[2] / running[1][..., None]
    return merged.reshape(rows_here, kv_heads * common_values * head_dim).astype(jnp.bfloat16)


def solution(mesh):
    return jax.shard_map(
        shards,
        mesh=mesh,
        in_specs=(
            P(("groups", "ctx"), ("head", "rep")),
            P(("groups", "ctx"), ("head", "rep")),
            P(("groups", "ctx"), ("head", "rep")),
            P(),
        ),
        out_specs=P(("groups", "ctx"), ("head", "rep")),
        check_vma=False,
    )
```

profile of v0, /device:TPU:0, one launch (start us, length us, event | category | flops | bytes accessed | tf_op | source)
XLA Modules:
  0.0 60.6 jit_solution(10825627206917604020)
XLA Ops:
  0.0 0.0 copy-start
  0.0 0.8 %select_reduce_fusion.1 = s32[256]{0:T(256)S(1)} fusion(s32[8]{0:T(128)} %param.9, s32[256]{0:T(256)S(1)} %and_select_fusion.2), kind=kLoop, calls=%fused_computation.45 | loop fusion | flops 5888 | bytes 2080 | tf_op jit(solution)/shard_map/reduce_sum | solution.py:15
  0.8 1.2 %copy.30 = bf16[256,1024]{0,1:T(8,128)(2,1)S(1)} copy(bf16[256,1024]{1,0:T(8,128)(2,1)} %param.6) | data formatting | bytes 1048576 | tf_op args[0]
  2.1 1.0 %copy.32 = bf16[256,2,4,128]{3,0,2,1:T(8,128)(2,1)} copy(bf16[256,2,4,128]{0,3,2,1:T(8,128)(2,1)S(1)} %bitcast.99) | data formatting | bytes 1048576
  3.1 17.6 %all_gather.6 = bf16[1024,256]{1,0:T(8,128)(2,1)S(1)} all-gather(bf16[256,256]{1,0:T(8,128)(2,1)} %param.7), channel_id=1, replica_groups=mesh['groups'=2,'ctx'=4,'head'=2,'rep'=2] {'ctx'}, dimensions={0}, use_global_device_ids=true | all-gather | bytes 655360 | tf_op jit(solution)/shard_map/all_gather | solution.py:69
  20.7 0.9 %reshape.66 = bf16[2,2,256,2,128]{4,3,2,1,0:T(2,128)(2,1)} reshape(bf16[1024,256]{1,0:T(8,128)(2,1)S(1)} %all_gather.6) | data formatting | bytes 1048576 | tf_op jit(solution)/shard_map/reshape | solution.py:75
  21.6 16.6 %all_gather.7 = bf16[1024,256]{1,0:T(8,128)(2,1)S(1)} all-gather(bf16[256,256]{1,0:T(8,128)(2,1)} %param.8), channel_id=1, replica_groups=mesh['groups'=2,'ctx'=4,'head'=2,'rep'=2] {'ctx'}, dimensions={0}, use_global_device_ids=true | all-gather | bytes 655360 | tf_op jit(solution)/shard_map/all_gather | solution.py:70
  38.2 0.9 %reshape.68 = bf16[2,2,256,2,128]{4,3,2,1,0:T(2,128)(2,1)} reshape(bf16[1024,256]{1,0:T(8,128)(2,1)S(1)} %all_gather.7) | data formatting | bytes 1048576 | tf_op jit(solution)/shard_map/reshape | solution.py:76
  39.1 0.0 copy-done
  39.1 0.1 select_reduce_fusion
  39.3 20.2 %while.15 = (s32[]{:T(128)}, f32[256,2,4]{0,2,1:T(4,128)S(1)}, f32[256,2,4]{0,2,1:T(4,128)S(1)}, f32[256,2,4,128]{0,3,2,1:T(8,128)S(1)}, s32[2,2,256]{2,1,0:T(2,...) while((s32[]{:T(128)}, f32[256,2,4]{0,2,1:T(4,128)S(1)}, ...), condition=%wide.region_5.6_spmd.clone, body=%wide.region_2.5_spmd.clone.sunk | while | flops 549871616 | bytes 19995776 | solution.py:87
  39.3 1.4 %constant_dynamic-slice_fusion.3 = (bf16[1,2,256,2,128]{4,3,2,1,0:T(2,128)(2,1)S(1)}, bf16[1,2,256,2,128]{4,3,2,1,0:T(2,128)(2,1)S(1)}) fusion(bf16[2,2,256,2,128]{4,3,2,1,0:T(2,128)(2,1)} %get-tuple-element.251, s32[]{:T(128)} %get-tuple-element.232, bf16[2,2,256,2,128]{4,3,2,1,0:T(2,128)(2,1)} %get-tuple-element.249), kind=kLoop, calls=%fused_computation.38.clone.1 | loop fusion | bytes 1048580 | tf_op jit(solution)/shard_map/while/body/jit(dynamic_index_in_dim)/dynamic_slice | solution.py:87
  40.7 0.1 broadcast_compare_fusion.3
  40.8 1.9 %fusion.43 = (f32[2,256,2,4]{1,3,0,2:T(4,128)S(1)}, f32[2,2,256,256,4]{3,2,4,1,0:T(8,128)S(1)}) fusion(pred[2,256,256]{1,2,0:T(8,128)(4,1)S(1)} %broadcast_compare_fusion.3, bf16[256,2,4,128]{3,0,2,1:T(8,128)(2,1)} %get-tuple-element.250, bf16[1,2,256,2,128]{4,3,2,1,0:T(2,128)(2,1)S(1)} %get-tuple-element.209), kind=kOutput, calls=%fused_computation.2.clone.1 | convolution fusion | flops 271577088 | bytes 5128192 | tf_op jit(solution)/shard_map/while/body/eval_jaxpr/rhgd,cshd->crhgs/dot_general | solution.py:24
  42.7 1.2 %fusion.44 = (bf16[2,256,2,4,256]{1,4,3,0,2:T(8,128)(2,1)S(1)}, f32[2,256,2,4]{1,3,0,2:T(4,128)S(1)}) fusion(f32[2,2,256,256,4]{3,2,4,1,0:T(8,128)S(1)} %get-tuple-element.211, f32[2,256,2,4]{1,3,0,2:T(4,128)S(1)} %get-tuple-element.210, pred[2,256,256]{1,2,0:T(8,128)(4,1)S(1)} %broadcast_compare_fusion.3), kind=kLoop, calls=%fused_computation.3.clone.1 | loop fusion | flops 6287360 | bytes 6455296 | tf_op jit(solution)/shard_map/while/body/eval_jaxpr/convert_element_type | solution.py:34
  43.9 0.9 %copy.63 = bf16[1,2,256,2,128]{2,4,3,1,0:T(8,128)(2,1)} copy(bf16[1,2,256,2,128]{4,3,2,1,0:T(2,128)(2,1)S(1)} %get-tuple-element.216) | data formatting | bytes 524288 | tf_op jit(solution)/shard_map/while/body/jit(dynamic_index_in_dim)/dynamic_slice | solution.py:87
  44.8 2.4 %fusion.46 = bf16[2,256,2,4,128]{1,4,3,2,0:T(8,128)(2,1)} fusion(bf16[2,256,2,4,256]{1,4,3,0,2:T(8,128)(2,1)S(1)} %get-tuple-element.215, bf16[1,2,256,2,128]{2,4,3,1,0:T(8,128)(2,1)} %copy.63, f32[2,256,2,4]{1,3,0,2:T(4,128)S(1)} %get-tuple-element.212), kind=kOutput, calls=%fused_computation.6.clone.1 | convolution fusion | flops 269488128 | bytes 3424256 | tf_op jit(solution)/shard_map/while/body/eval_jaxpr/crhgs,cshd->crhgd/dot_general | solution.py:32
  47.2 2.1 %fusion.47 = f32[256,2,4,128]{0,3,2,1:T(8,128)S(1)} fusion(f32[256,2,4,128]{0,3,2,1:T(8,128)S(1)} %get-tuple-element.235, bf16[2,256,2,4,128]{1,4,3,2,0:T(8,128)(2,1)} %fusion.46, f32[256,2,4]{0,2,1:T(4,128)S(1)} %get-tuple-element.217, f32[256,2,4]{0,2,1:T(4,128)S(1)} %get-tuple-element.218, f32[256,2,4]{0,2,1:T(4,128)S(1)} %get-tuple-element.219, ...), kind=kLoop, calls=%fused_computation.10.clone.1 | loop fusion | flops 2359296 | bytes 3178497 | tf_op jit(solution)/shard_map/while/body/eval_jaxpr/add | solution.py:50
  49.4 1.4 %constant_dynamic-slice_fusion.3 = (bf16[1,2,256,2,128]{4,3,2,1,0:T(2,128)(2,1)S(1)}, bf16[1,2,256,2,128]{4,3,2,1,0:T(2,128)(2,1)S(1)}) fusion(bf16[2,2,256,2,128]{4,3,2,1,0:T(2,128)(2,1)} %get-tuple-element.251, s32[]{:T(128)} %get-tuple-element.232, bf16[2,2,256,2,128]{4,3,2,1,0:T(2,128)(2,1)} %get-tuple-element.249), kind=kLoop, calls=%fused_computation.38.clone.1 | loop fusion | bytes 1048580 | tf_op jit(solution)/shard_map/while/body/jit(dynamic_index_in_dim)/dynamic_slice | solution.py:87
  50.8 0.1 broadcast_compare_fusion.3
  50.9 1.9 %fusion.43 = (f32[2,256,2,4]{1,3,0,2:T(4,128)S(1)}, f32[2,2,256,256,4]{3,2,4,1,0:T(8,128)S(1)}) fusion(pred[2,256,256]{1,2,0:T(8,128)(4,1)S(1)} %broadcast_compare_fusion.3, bf16[256,2,4,128]{3,0,2,1:T(8,128)(2,1)} %get-tuple-element.250, bf16[1,2,256,2,128]{4,3,2,1,0:T(2,128)(2,1)S(1)} %get-tuple-element.209), kind=kOutput, calls=%fused_computation.2.clone.1 | convolution fusion | flops 271577088 | bytes 5128192 | tf_op jit(solution)/shard_map/while/body/eval_jaxpr/rhgd,cshd->crhgs/dot_general | solution.py:24
  52.8 1.2 %fusion.44 = (bf16[2,256,2,4,256]{1,4,3,0,2:T(8,128)(2,1)S(1)}, f32[2,256,2,4]{1,3,0,2:T(4,128)S(1)}) fusion(f32[2,2,256,256,4]{3,2,4,1,0:T(8,128)S(1)} %get-tuple-element.211, f32[2,256,2,4]{1,3,0,2:T(4,128)S(1)} %get-tuple-element.210, pred[2,256,256]{1,2,0:T(8,128)(4,1)S(1)} %broadcast_compare_fusion.3), kind=kLoop, calls=%fused_computation.3.clone.1 | loop fusion | flops 6287360 | bytes 6455296 | tf_op jit(solution)/shard_map/while/body/eval_jaxpr/convert_element_type | solution.py:34
  54.0 0.9 %copy.63 = bf16[1,2,256,2,128]{2,4,3,1,0:T(8,128)(2,1)} copy(bf16[1,2,256,2,128]{4,3,2,1,0:T(2,128)(2,1)S(1)} %get-tuple-element.216) | data formatting | bytes 524288 | tf_op jit(solution)/shard_map/while/body/jit(dynamic_index_in_dim)/dynamic_slice | solution.py:87
  54.9 2.4 %fusion.46 = bf16[2,256,2,4,128]{1,4,3,2,0:T(8,128)(2,1)} fusion(bf16[2,256,2,4,256]{1,4,3,0,2:T(8,128)(2,1)S(1)} %get-tuple-element.215, bf16[1,2,256,2,128]{2,4,3,1,0:T(8,128)(2,1)} %copy.63, f32[2,256,2,4]{1,3,0,2:T(4,128)S(1)} %get-tuple-element.212), kind=kOutput, calls=%fused_computation.6.clone.1 | convolution fusion | flops 269488128 | bytes 3424256 | tf_op jit(solution)/shard_map/while/body/eval_jaxpr/crhgs,cshd->crhgd/dot_general | solution.py:32
  57.3 2.1 %fusion.47 = f32[256,2,4,128]{0,3,2,1:T(8,128)S(1)} fusion(f32[256,2,4,128]{0,3,2,1:T(8,128)S(1)} %get-tuple-element.235, bf16[2,256,2,4,128]{1,4,3,2,0:T(8,128)(2,1)} %fusion.46, f32[256,2,4]{0,2,1:T(4,128)S(1)} %get-tuple-element.217, f32[256,2,4]{0,2,1:T(4,128)S(1)} %get-tuple-element.218, f32[256,2,4]{0,2,1:T(4,128)S(1)} %get-tuple-element.219, ...), kind=kLoop, calls=%fused_computation.10.clone.1 | loop fusion | flops 2359296 | bytes 3178497 | tf_op jit(solution)/shard_map/while/body/eval_jaxpr/add | solution.py:50
  59.5 0.1 divide_convert_fusion
  59.6 1.0 %copy.39 = bf16[256,1024]{1,0:T(8,128)(2,1)} copy(bf16[256,1024]{0,1:T(8,128)(2,1)S(1)} %bitcast.98) | data formatting | bytes 1048576 | tf_op jit(solution)/shard_map/convert_element_type | solution.py:89
  (13 shorter events, 0.1 us)
Async XLA Ops:
  0.0 39.1 %copy-start = (s32[8]{0:T(128)S(1)}, s32[8]{0:T(128)}, u32[]{:S(2)}) copy-start(s32[8]{0:T(128)} %param.9) | copy-start | bytes 100
where the time goes:
time: 61 us; the launch traced here: 60.6 us
  blocking collectives  34.1 us (56%)
  local copies, waits for them, and re-layouts  9.69 us (16%)
  matrix products  8.65 us (14%)
  other arithmetic  7.94 us (13%)
    all_gather x1, blocking collectives, shards(): k_piece = lax.all_gather(keys, 'ctx', axis=0, tiled=True)  17.6 us
    all_gather x1, blocking collectives, shards(): v_piece = lax.all_gather(values, 'ctx', axis=0, tiled=True)  16.6 us
    dot_general x2, matrix products, source_partials(): jnp.einsum('crhgs,cshd->crhgd', weights.astype(jnp.bfloat16), value_group...  4.85 us
    dynamic_slice x4, local copies, waits for them, and re-layouts, shards(): running, unused = lax.scan(one_turn, running, (k_steps, v_steps, p_steps))  4.53 us
    add x2, other arithmetic, absorb(): run_sum * rescale[..., None]  4.23 us
    dot_general x2, matrix products, source_partials(): jnp.einsum('rhgd,cshd->crhgs', query_block, key_group, preferred_element_...  3.8 us
    convert_element_type x2, other arithmetic, source_partials(): weights.astype(jnp.bfloat16)  2.34 us
    unnamed x4, local copies, waits for them, and re-layouts  2.27 us

commit v1 on v0

--- a/solution.py
+++ b/solution.py
@@ -67,7 +67,12 @@
     )
     running = initial
     k_piece = lax.all_gather(keys, "ctx", axis=0, tiled=True)
-    v_piece = lax.all_gather(values, "ctx", axis=0, tiled=True)
+    ring = [values]
+    for hop in range(3):
+        ring.append(lax.ppermute(ring[-1], "ctx", [(dev, (dev + 1) % 4) for dev in range(4)]))
+    v_piece = jnp.roll(
+        jnp.concatenate(ring[::-1], axis=0), (lax.axis_index("ctx") + 1) * ring[0].shape[0], axis=0
+    )
     shard_count = k_piece.shape[0] // rows_here
     per_turn = 2
     turn_count = shard_count // per_turn

time: 61 us -> 56.3 us (0.923)
  blocking collectives: 34.1 us -> 16.1 us
  waiting for transfers between devices: 0 us -> 9.51 us
  starting transfers between devices: 0 us -> 3.06 us
    all_gather x1 -> x0, blocking collectives: 16.6 us -> none  [shards(): v_piece = lax.all_gather(values, 'ctx', axis=0, tiled=True)]
    ppermute x0 -> x3, waiting for transfers between devices: none -> 9.51 us  [shards(): lax.ppermute(ring[-1], 'ctx', [(dev, (dev + 1) % 4) for dev in range(4)])]
    ppermute x0 -> x3, starting transfers between devices: none -> 3.06 us  [shards(): lax.ppermute(ring[-1], 'ctx', [(dev, (dev + 1) % 4) for dev in range(4)])]
    all_gather x1, blocking collectives: 17.6 us -> 16.1 us  [shards(): k_piece = lax.all_gather(keys, 'ctx', axis=0, tiled=True)]
    unnamed x4 -> x11, local copies, waits for them, and re-layouts: 2.27 us -> 2.35 us
  transfers between devices with their start and end apart: 0 -> 3, of which waited for: 0 -> 2; matrix products, arithmetic and copies ran while one was open for 0% -> 8% of each run, Pallas kernels for 0% -> 0%
where the time goes in v1:
time: 56.3 us; the launch traced here: 55.9 us
  blocking collectives  16.1 us (29%)
  local copies, waits for them, and re-layouts  9.82 us (17%)
  waiting for transfers between devices  9.51 us (17%)
  matrix products  8.65 us (15%)
  other arithmetic  8.54 us (15%)
  starting transfers between devices  3.06 us (5%)
    all_gather x1, blocking collectives, shards(): k_piece = lax.all_gather(keys, 'ctx', axis=0, tiled=True)  16.1 us
    ppermute x3, waiting for transfers between devices, shards(): lax.ppermute(ring[-1], 'ctx', [(dev, (dev + 1) % 4) for dev in range(4)])  9.51 us
    dot_general x2, matrix products, source_partials(): jnp.einsum('crhgs,cshd->crhgd', weights.astype(jnp.bfloat16), value_group...  4.85 us
    dynamic_slice x4, local copies, waits for them, and re-layouts, shards(): running, unused = lax.scan(one_turn, running, (k_steps, v_steps, p_steps))  4.53 us
    add x2, other arithmetic, absorb(): run_sum * rescale[..., None]  4.23 us
    dot_general x2, matrix products, source_partials(): jnp.einsum('rhgd,cshd->crhgs', query_block, key_group, preferred_element_...  3.8 us
    ppermute x3, starting transfers between devices, shards(): lax.ppermute(ring[-1], 'ctx', [(dev, (dev + 1) % 4) for dev in range(4)])  3.06 us
    unnamed x11, local copies, waits for them, and re-layouts  2.35 us
  transfers between devices with their start and end apart: 3, of which 2 were waited for; matrix products, arithmetic and copies ran while one was open for 8% of the time, Pallas kernels for 0%

profile of v1, /device:TPU:0, one launch (start us, length us, event | category | flops | bytes accessed | tf_op | source)
XLA Modules:
  0.0 55.9 jit_solution(2914489114047905728)
XLA Ops:
  0.0 0.0 copy-start
  0.0 3.1 %collective-permute-start = (bf16[256,256]{1,0:T(8,128)(2,1)}, bf16[256,256]{1,0:T(8,128)(2,1)S(1)}, u32[]{:S(2)}, u32[]{:S(2)}) collective-permute-start(bf16[256,256]{1,0:T(8,128)(2,1)} %param.8), channel_id=1, source_target_pairs={{0,4},{4,8},{8,12},{12,0},{1,5},{5,9},{9,13},{13,1},{2,6},{6,10},{... | collective-permute-start | bytes 393224 | tf_op jit(solution)/shard_map/ppermute | solution.py:72
  3.1 0.7 %select_reduce_fusion = s32[1024]{0:T(1024)S(1)} fusion(s32[8]{0:T(128)} %param.9, s32[1024]{0:T(1024)S(1)} %add_select_fusion), kind=kLoop, calls=%fused_computation.41 | loop fusion | flops 23552 | bytes 8224 | tf_op jit(solution)/shard_map/reduce_sum | solution.py:15
  3.8 16.1 %all_gather.3 = bf16[1024,256]{1,0:T(8,128)(2,1)S(1)} all-gather(bf16[256,256]{1,0:T(8,128)(2,1)} %param.7), channel_id=1, replica_groups=mesh['groups'=2,'ctx'=4,'head'=2,'rep'=2] {'ctx'}, dimensions={0}, use_global_device_ids=true | all-gather | bytes 655360 | tf_op jit(solution)/shard_map/all_gather | solution.py:69
  19.9 0.0 collective-permute-done
  19.9 0.0 collective-permute-start.1
  20.0 1.2 %copy.30 = bf16[256,1024]{0,1:T(8,128)(2,1)S(1)} copy(bf16[256,1024]{1,0:T(8,128)(2,1)} %param.6) | data formatting | bytes 1048576 | tf_op args[0]
  21.2 1.0 %copy.32 = bf16[256,2,4,128]{3,0,2,1:T(8,128)(2,1)} copy(bf16[256,2,4,128]{0,3,2,1:T(8,128)(2,1)S(1)} %bitcast.99) | data formatting | bytes 1048576
  22.3 0.9 %reshape.66 = bf16[2,2,256,2,128]{4,3,2,1,0:T(2,128)(2,1)} reshape(bf16[1024,256]{1,0:T(8,128)(2,1)S(1)} %all_gather.3) | data formatting | bytes 1048576 | tf_op jit(solution)/shard_map/reshape | solution.py:80
  23.2 0.7 %select_reduce_fusion.1 = s32[256]{0:T(256)S(1)} fusion(s32[8]{0:T(128)} %param.9, s32[256]{0:T(256)S(1)} %and_select_fusion.2), kind=kLoop, calls=%fused_computation.53 | loop fusion | flops 5888 | bytes 2080 | tf_op jit(solution)/shard_map/reduce_sum | solution.py:15
  23.9 2.8 %collective-permute-done.1 = bf16[256,256]{1,0:T(8,128)(2,1)S(1)} collective-permute-done((bf16[256,256]{1,0:T(8,128)(2,1)S(1)}, bf16[256,256]{1,0:T(8,128)(2,1)S(1)}, u32[]{:S(2)}, u32[]{:S(2)}) %collective-permute-start.1) | collective-permute-done | bytes 131104 | tf_op jit(solution)/shard_map/ppermute | solution.py:72
  26.7 0.0 collective-permute-start.2
  26.7 6.8 %collective-permute-done.2 = bf16[256,256]{1,0:T(8,128)(2,1)S(1)} collective-permute-done((bf16[256,256]{1,0:T(8,128)(2,1)S(1)}, bf16[256,256]{1,0:T(8,128)(2,1)S(1)}, u32[]{:S(2)}, u32[]{:S(2)}) %collective-permute-start.2) | collective-permute-done | bytes 131104 | tf_op jit(solution)/shard_map/ppermute | solution.py:72
  33.5 0.0 copy-done
  33.6 0.9 %reshape.68 = bf16[2,2,256,2,128]{4,3,2,1,0:T(2,128)(2,1)} reshape(bf16[1024,256]{1,0:T(8,128)(2,1)S(1)} %constant_dynamic-slice_fusion.2) | data formatting | bytes 1048576 | tf_op jit(solution)/shard_map/reshape | solution.py:81
  34.6 20.2 %while.15 = (s32[]{:T(128)}, f32[256,2,4]{0,2,1:T(4,128)S(1)}, f32[256,2,4]{0,2,1:T(4,128)S(1)}, f32[256,2,4,128]{0,3,2,1:T(8,128)S(1)}, s32[2,2,256]{2,1,0:T(2,...) while((s32[]{:T(128)}, f32[256,2,4]{0,2,1:T(4,128)S(1)}, ...), condition=%wide.region_5.6_spmd.clone, body=%wide.region_2.5_spmd.clone.sunk | while | flops 549871616 | bytes 19995776 | solution.py:92
  34.6 1.4 %constant_dynamic-slice_fusion.4 = (bf16[1,2,256,2,128]{4,3,2,1,0:T(2,128)(2,1)S(1)}, bf16[1,2,256,2,128]{4,3,2,1,0:T(2,128)(2,1)S(1)}) fusion(bf16[2,2,256,2,128]{4,3,2,1,0:T(2,128)(2,1)} %get-tuple-element.251, s32[]{:T(128)} %get-tuple-element.232, bf16[2,2,256,2,128]{4,3,2,1,0:T(2,128)(2,1)} %get-tuple-element.249), kind=kLoop, calls=%fused_computation.38.clone.1 | loop fusion | bytes 1048580 | tf_op jit(solution)/shard_map/while/body/jit(dynamic_index_in_dim)/dynamic_slice | solution.py:92
  36.0 0.1 broadcast_compare_fusion.3
  36.1 1.9 %fusion.43 = (f32[2,256,2,4]{1,3,0,2:T(4,128)S(1)}, f32[2,2,256,256,4]{3,2,4,1,0:T(8,128)S(1)}) fusion(pred[2,256,256]{1,2,0:T(8,128)(4,1)S(1)} %broadcast_compare_fusion.3, bf16[256,2,4,128]{3,0,2,1:T(8,128)(2,1)} %get-tuple-element.250, bf16[1,2,256,2,128]{4,3,2,1,0:T(2,128)(2,1)S(1)} %get-tuple-element.209), kind=kOutput, calls=%fused_computation.2.clone.1 | convolution fusion | flops 271577088 | bytes 5128192 | tf_op jit(solution)/shard_map/while/body/eval_jaxpr/rhgd,cshd->crhgs/dot_general | solution.py:24
  38.0 1.2 %fusion.44 = (bf16[2,256,2,4,256]{1,4,3,0,2:T(8,128)(2,1)S(1)}, f32[2,256,2,4]{1,3,0,2:T(4,128)S(1)}) fusion(f32[2,2,256,256,4]{3,2,4,1,0:T(8,128)S(1)} %get-tuple-element.211, f32[2,256,2,4]{1,3,0,2:T(4,128)S(1)} %get-tuple-element.210, pred[2,256,256]{1,2,0:T(8,128)(4,1)S(1)} %broadcast_compare_fusion.3), kind=kLoop, calls=%fused_computation.3.clone.1 | loop fusion | flops 6287360 | bytes 6455296 | tf_op jit(solution)/shard_map/while/body/eval_jaxpr/convert_element_type | solution.py:34
  39.2 0.9 %copy.63 = bf16[1,2,256,2,128]{2,4,3,1,0:T(8,128)(2,1)} copy(bf16[1,2,256,2,128]{4,3,2,1,0:T(2,128)(2,1)S(1)} %get-tuple-element.216) | data formatting | bytes 524288 | tf_op jit(solution)/shard_map/while/body/jit(dynamic_index_in_dim)/dynamic_slice | solution.py:92
  40.1 2.4 %fusion.46 = bf16[2,256,2,4,128]{1,4,3,2,0:T(8,128)(2,1)} fusion(bf16[2,256,2,4,256]{1,4,3,0,2:T(8,128)(2,1)S(1)} %get-tuple-element.215, bf16[1,2,256,2,128]{2,4,3,1,0:T(8,128)(2,1)} %copy.63, f32[2,256,2,4]{1,3,0,2:T(4,128)S(1)} %get-tuple-element.212), kind=kOutput, calls=%fused_computation.6.clone.1 | convolution fusion | flops 269488128 | bytes 3424256 | tf_op jit(solution)/shard_map/while/body/eval_jaxpr/crhgs,cshd->crhgd/dot_general | solution.py:32
  42.5 2.1 %fusion.47 = f32[256,2,4,128]{0,3,2,1:T(8,128)S(1)} fusion(f32[256,2,4,128]{0,3,2,1:T(8,128)S(1)} %get-tuple-element.235, bf16[2,256,2,4,128]{1,4,3,2,0:T(8,128)(2,1)} %fusion.46, f32[256,2,4]{0,2,1:T(4,128)S(1)} %get-tuple-element.217, f32[256,2,4]{0,2,1:T(4,128)S(1)} %get-tuple-element.218, f32[256,2,4]{0,2,1:T(4,128)S(1)} %get-tuple-element.219, ...), kind=kLoop, calls=%fused_computation.10.clone.1 | loop fusion | flops 2359296 | bytes 3178497 | tf_op jit(solution)/shard_map/while/body/eval_jaxpr/add | solution.py:50
  44.7 1.4 %constant_dynamic-slice_fusion.4 = (bf16[1,2,256,2,128]{4,3,2,1,0:T(2,128)(2,1)S(1)}, bf16[1,2,256,2,128]{4,3,2,1,0:T(2,128)(2,1)S(1)}) fusion(bf16[2,2,256,2,128]{4,3,2,1,0:T(2,128)(2,1)} %get-tuple-element.251, s32[]{:T(128)} %get-tuple-element.232, bf16[2,2,256,2,128]{4,3,2,1,0:T(2,128)(2,1)} %get-tuple-element.249), kind=kLoop, calls=%fused_computation.38.clone.1 | loop fusion | bytes 1048580 | tf_op jit(solution)/shard_map/while/body/jit(dynamic_index_in_dim)/dynamic_slice | solution.py:92
  46.1 0.1 broadcast_compare_fusion.3
  46.2 1.9 %fusion.43 = (f32[2,256,2,4]{1,3,0,2:T(4,128)S(1)}, f32[2,2,256,256,4]{3,2,4,1,0:T(8,128)S(1)}) fusion(pred[2,256,256]{1,2,0:T(8,128)(4,1)S(1)} %broadcast_compare_fusion.3, bf16[256,2,4,128]{3,0,2,1:T(8,128)(2,1)} %get-tuple-element.250, bf16[1,2,256,2,128]{4,3,2,1,0:T(2,128)(2,1)S(1)} %get-tuple-element.209), kind=kOutput, calls=%fused_computation.2.clone.1 | convolution fusion | flops 271577088 | bytes 5128192 | tf_op jit(solution)/shard_map/while/body/eval_jaxpr/rhgd,cshd->crhgs/dot_general | solution.py:24
  48.1 1.2 %fusion.44 = (bf16[2,256,2,4,256]{1,4,3,0,2:T(8,128)(2,1)S(1)}, f32[2,256,2,4]{1,3,0,2:T(4,128)S(1)}) fusion(f32[2,2,256,256,4]{3,2,4,1,0:T(8,128)S(1)} %get-tuple-element.211, f32[2,256,2,4]{1,3,0,2:T(4,128)S(1)} %get-tuple-element.210, pred[2,256,256]{1,2,0:T(8,128)(4,1)S(1)} %broadcast_compare_fusion.3), kind=kLoop, calls=%fused_computation.3.clone.1 | loop fusion | flops 6287360 | bytes 6455296 | tf_op jit(solution)/shard_map/while/body/eval_jaxpr/convert_element_type | solution.py:34
  49.3 0.9 %copy.63 = bf16[1,2,256,2,128]{2,4,3,1,0:T(8,128)(2,1)} copy(bf16[1,2,256,2,128]{4,3,2,1,0:T(2,128)(2,1)S(1)} %get-tuple-element.216) | data formatting | bytes 524288 | tf_op jit(solution)/shard_map/while/body/jit(dynamic_index_in_dim)/dynamic_slice | solution.py:92
  50.2 2.4 %fusion.46 = bf16[2,256,2,4,128]{1,4,3,2,0:T(8,128)(2,1)} fusion(bf16[2,256,2,4,256]{1,4,3,0,2:T(8,128)(2,1)S(1)} %get-tuple-element.215, bf16[1,2,256,2,128]{2,4,3,1,0:T(8,128)(2,1)} %copy.63, f32[2,256,2,4]{1,3,0,2:T(4,128)S(1)} %get-tuple-element.212), kind=kOutput, calls=%fused_computation.6.clone.1 | convolution fusion | flops 269488128 | bytes 3424256 | tf_op jit(solution)/shard_map/while/body/eval_jaxpr/crhgs,cshd->crhgd/dot_general | solution.py:32
  52.6 2.1 %fusion.47 = f32[256,2,4,128]{0,3,2,1:T(8,128)S(1)} fusion(f32[256,2,4,128]{0,3,2,1:T(8,128)S(1)} %get-tuple-element.235, bf16[2,256,2,4,128]{1,4,3,2,0:T(8,128)(2,1)} %fusion.46, f32[256,2,4]{0,2,1:T(4,128)S(1)} %get-tuple-element.217, f32[256,2,4]{0,2,1:T(4,128)S(1)} %get-tuple-element.218, f32[256,2,4]{0,2,1:T(4,128)S(1)} %get-tuple-element.219, ...), kind=kLoop, calls=%fused_computation.10.clone.1 | loop fusion | flops 2359296 | bytes 3178497 | tf_op jit(solution)/shard_map/while/body/eval_jaxpr/add | solution.py:50
  54.8 0.1 divide_convert_fusion
  54.9 1.0 %copy.39 = bf16[256,1024]{1,0:T(8,128)(2,1)} copy(bf16[256,1024]{0,1:T(8,128)(2,1)S(1)} %bitcast.98) | data formatting | bytes 1048576 | tf_op jit(solution)/shard_map/convert_element_type | solution.py:94
  (22 shorter events, 0.3 us)
Async XLA Ops:
  0.0 33.5 %copy-start = (bf16[256,256]{1,0:T(8,128)(2,1)S(1)}, bf16[256,256]{1,0:T(8,128)(2,1)}, u32[]{:S(2)}) copy-start(bf16[256,256]{1,0:T(8,128)(2,1)} %param.8) | copy-start | bytes 393220
  0.0 19.9 %collective-permute-start = (bf16[256,256]{1,0:T(8,128)(2,1)}, bf16[256,256]{1,0:T(8,128)(2,1)S(1)}, u32[]{:S(2)}, u32[]{:S(2)}) collective-permute-start(bf16[256,256]{1,0:T(8,128)(2,1)} %param.8), channel_id=1, source_target_pairs={{0,4},{4,8},{8,12},{12,0},{1,5},{5,9},{9,13},{13,1},{2,6},{6,10},{... | collective-permute-start | bytes 393224 | tf_op jit(solution)/shard_map/ppermute | solution.py:72
  19.9 6.8 %collective-permute-start.1 = (bf16[256,256]{1,0:T(8,128)(2,1)S(1)}, bf16[256,256]{1,0:T(8,128)(2,1)S(1)}, u32[]{:S(2)}, u32[]{:S(2)}) collective-permute-start(bf16[256,256]{1,0:T(8,128)(2,1)S(1)} %collective-permute-done), channel_id=1, source_target_pairs={{0,4},{4,8},{8,12},{12,0},{1,5},{5,9},{9,13},{13,1},{2,6},{6,10},{... | collective-permute-start | bytes 393224 | tf_op jit(solution)/shard_map/ppermute | solution.py:72
  26.7 6.8 %collective-permute-start.2 = (bf16[256,256]{1,0:T(8,128)(2,1)S(1)}, bf16[256,256]{1,0:T(8,128)(2,1)S(1)}, u32[]{:S(2)}, u32[]{:S(2)}) collective-permute-start(bf16[256,256]{1,0:T(8,128)(2,1)S(1)} %collective-permute-done.1), channel_id=1, source_target_pairs={{0,4},{4,8},{8,12},{12,0},{1,5},{5,9},{9,13},{13,1},{2,6},{6,10},{... | collective-permute-start | bytes 393224 | tf_op jit(solution)/shard_map/ppermute | solution.py:72
